TPU v7x, 32 devices: a whole 2x2x4 slice. The times are simulated.
32 devices in a mesh: seq: 8 (over z, y), rep: 4 (over x, core).
Axes of the slice: x: 2, y: 2, z: 4, core: 2. Of those that a mesh axis runs over, the one named last changes fastest.
Arguments:
- head_out: bfloat16 [4, 4096, 4096], P('rep', 'seq'), may hold values from -6 to 6
- grad_out: bfloat16 [4, 4096, 3584], P('rep', 'seq'), may hold values from -6 to 6
- hash_codes: int32 [4, 16, 3584], P('rep'), may hold values from 0 to 511
- loss_mask: int32 [4096], P('seq'), may hold values 0 or 1
- query_ids: int32 [64], replicated, may hold values from 0 to 4095
Outputs:
- attribution: float32 [4096, 64], P(('seq', 'rep'))
All inputs are finite; a program needn't handle non-finite values. No bound on the sum of `loss_mask` on one device may be relied on, other than what follows from the above.
Results may differ from a plain program's by a relative error of at most 0.0025.
Values may be sent and summed in bfloat16 or wider, within the bound.
A program may use at most 64 MiB of HBM per device.

v0:
```python
import math
import jax
import jax.numpy as jnp
from jax import lax
from jax.sharding import PartitionSpec as P

ridge_shift = 0.25
norm_floor = 1e-06


def build_sketches(outputs, gradient, codes):
    head_count = codes.shape[0]
    sketch_width = outputs.shape[1] // head_count
    model_width = gradient.shape[1]
    sketch_scale = math.sqrt(sketch_width / model_width)
    columns = jnp.arange(sketch_width, dtype=jnp.int32)

    def one_head(head_index):
        head_codes = codes[head_index]
        bucket = head_codes % sketch_width
        sign_flip = 1 - 2 * (head_codes // sketch_width)
        count_table = jnp.where(bucket[:, None] == columns[None, :], sign_flip[:, None], 0).astype(
            jnp.bfloat16
        )
        counted = jnp.dot(gradient, count_table, preferred_element_type=jnp.float32)
        picked = lax.dynamic_slice_in_dim(
            outputs, head_index * sketch_width, sketch_width, 1
        ).astype(jnp.float32)
        return (picked * counted * sketch_scale).astype(jnp.bfloat16)

    return lax.map(one_head, jnp.arange(head_count, dtype=jnp.int32))


def solve_queries(gram_sum, chosen, token_count):
    sketch_width = gram_sum.shape[0]
    gram_sum = gram_sum / token_count + ridge_shift * jnp.eye(sketch_width, dtype=jnp.float32)
    factor = jnp.linalg.cholesky(gram_sum)
    return jax.scipy.linalg.cho_solve((factor, True), chosen.T).astype(jnp.bfloat16)


def on_device(head_out, grad_out, hash_codes, loss_mask, query_ids):
    sketches = build_sketches(head_out[0], grad_out[0], hash_codes[0])
    tok_rows = loss_mask.shape[0]
    out_rows = tok_rows // lax.axis_size("rep")
    mask_bf = loss_mask.astype(jnp.bfloat16)
    local_count = jnp.sum(loss_mask.astype(jnp.float32))
    token_count = lax.psum(local_count, "seq") + 1.0
    local_grams = jnp.einsum(
        "htk,htj->hkj",
        sketches * mask_bf[None, :, None],
        sketches,
        preferred_element_type=jnp.float32,
    )
    first_row = lax.axis_index("seq") * tok_rows
    query_hits = (
        query_ids[:, None] - first_row == jnp.arange(tok_rows, dtype=jnp.int32)[None, :]
    ).astype(jnp.bfloat16)
    local_chosen = jnp.einsum(
        "qt,htk->hqk", query_hits, sketches, preferred_element_type=jnp.float32
    )
    own_grams, own_chosen = (
        lax.psum_scatter(local_grams, "seq", scatter_dimension=0, tiled=True),
        lax.psum_scatter(local_chosen, "seq", scatter_dimension=0, tiled=True),
    )
    solved = jnp.stack(
        [
            solve_queries(own_grams[slot_index], own_chosen[slot_index], token_count)
            for slot_index in range(own_grams.shape[0])
        ]
    )
    solved_all = lax.all_gather(solved, "seq", axis=0, tiled=True)
    score_sum = jnp.einsum("htk,hkq->tq", sketches, solved_all, preferred_element_type=jnp.float32)
    contrib = lax.psum_scatter(score_sum, "rep", scatter_dimension=0, tiled=True)
    row_start = lax.axis_index("rep") * out_rows
    mask_rows = lax.dynamic_slice_in_dim(loss_mask, row_start, out_rows, 0).astype(jnp.float32)
    partial_value = jnp.sum(mask_rows[:, None] * contrib * contrib, 0)
    norm_sum = lax.psum(partial_value, ("seq", "rep")) / token_count
    return contrib / jnp.sqrt(norm_sum + norm_floor)


def solution(mesh):
    placed = (P("rep", "seq", None), P("rep", "seq", None), P("rep", None, None), P("seq"), P())
    return jax.shard_map(
        on_device, mesh=mesh, in_specs=placed, out_specs=P(("seq", "rep"), None), check_vma=False
    )
```

profile of v0, /device:TPU:0, one launch (start us, length us, event | category | flops | bytes accessed | tf_op | source)
XLA Modules:
  0.0 561.4 jit_solution(14292173351317738377)
XLA Ops:
  6.5 6.5 %copy.13 = bf16[1,512,4096]{1,2,0:T(8,128)(2,1)} copy(bf16[1,512,4096]{2,1,0:T(8,128)(2,1)} %param.10) | data formatting | bytes 8388608 | tf_op args[0]
  13.0 158.3 %while.17 = (s32[]{:T(128)}, bf16[16,512,256]{1,2,0:T(8,128)(2,1)}, s32[16]{0:T(128)S(1)}, bf16[512,4096]{0,1:T(8,128)(2,1)}, s32[16,3584]{1,0:T(8,128)}, /*inde...) while((s32[]{:T(128)}, bf16[16,512,256]{1,2,0:T(8,128)(2,1)}, ...), condition=%wide.region_1.2_spmd.clone, body=%wide.region_0.1_spmd.clone.sunk | while | flops 942876160 | bytes 4295377 | solution.py:31
  15.8 0.9 dynamic-slice_reduce_fusion.2
  16.8 6.1 %fusion.76 = bf16[16,512,256]{1,2,0:T(8,128)(2,1)} fusion(bf16[16,512,256]{1,2,0:T(8,128)(2,1)} %get-tuple-element.293, s32[]{:T(128)} %get-tuple-element.292, bf16[512,3584]{1,0:T(8,128)(2,1)} %get-tuple-element.308, s32[3584]{0:T(1024)S(1)} %get-tuple-element.267, s32[3584]{0:T(1024)S(1)} %get-tuple-element.268, ...), kind=kOutput, calls=%fused_computation.16.clone.1 | convolution fusion | flops 942800896 | bytes 4223492 | tf_op jit(solution)/shard_map/while/body/eval_jaxpr/dot_general | solution.py:25
  25.7 0.9 dynamic-slice_reduce_fusion.2
  26.7 6.1 %fusion.76 = bf16[16,512,256]{1,2,0:T(8,128)(2,1)} fusion(bf16[16,512,256]{1,2,0:T(8,128)(2,1)} %get-tuple-element.293, s32[]{:T(128)} %get-tuple-element.292, bf16[512,3584]{1,0:T(8,128)(2,1)} %get-tuple-element.308, s32[3584]{0:T(1024)S(1)} %get-tuple-element.267, s32[3584]{0:T(1024)S(1)} %get-tuple-element.268, ...), kind=kOutput, calls=%fused_computation.16.clone.1 | convolution fusion | flops 942800896 | bytes 4223492 | tf_op jit(solution)/shard_map/while/body/eval_jaxpr/dot_general | solution.py:25
  35.6 0.9 dynamic-slice_reduce_fusion.2
  36.6 6.1 %fusion.76 = bf16[16,512,256]{1,2,0:T(8,128)(2,1)} fusion(bf16[16,512,256]{1,2,0:T(8,128)(2,1)} %get-tuple-element.293, s32[]{:T(128)} %get-tuple-element.292, bf16[512,3584]{1,0:T(8,128)(2,1)} %get-tuple-element.308, s32[3584]{0:T(1024)S(1)} %get-tuple-element.267, s32[3584]{0:T(1024)S(1)} %get-tuple-element.268, ...), kind=kOutput, calls=%fused_computation.16.clone.1 | convolution fusion | flops 942800896 | bytes 4223492 | tf_op jit(solution)/shard_map/while/body/eval_jaxpr/dot_general | solution.py:25
  45.5 0.9 dynamic-slice_reduce_fusion.2
  46.5 6.1 %fusion.76 = bf16[16,512,256]{1,2,0:T(8,128)(2,1)} fusion(bf16[16,512,256]{1,2,0:T(8,128)(2,1)} %get-tuple-element.293, s32[]{:T(128)} %get-tuple-element.292, bf16[512,3584]{1,0:T(8,128)(2,1)} %get-tuple-element.308, s32[3584]{0:T(1024)S(1)} %get-tuple-element.267, s32[3584]{0:T(1024)S(1)} %get-tuple-element.268, ...), kind=kOutput, calls=%fused_computation.16.clone.1 | convolution fusion | flops 942800896 | bytes 4223492 | tf_op jit(solution)/shard_map/while/body/eval_jaxpr/dot_general | solution.py:25
  55.4 0.9 dynamic-slice_reduce_fusion.2
  56.4 6.1 %fusion.76 = bf16[16,512,256]{1,2,0:T(8,128)(2,1)} fusion(bf16[16,512,256]{1,2,0:T(8,128)(2,1)} %get-tuple-element.293, s32[]{:T(128)} %get-tuple-element.292, bf16[512,3584]{1,0:T(8,128)(2,1)} %get-tuple-element.308, s32[3584]{0:T(1024)S(1)} %get-tuple-element.267, s32[3584]{0:T(1024)S(1)} %get-tuple-element.268, ...), kind=kOutput, calls=%fused_computation.16.clone.1 | convolution fusion | flops 942800896 | bytes 4223492 | tf_op jit(solution)/shard_map/while/body/eval_jaxpr/dot_general | solution.py:25
  65.3 0.9 dynamic-slice_reduce_fusion.2
  66.3 6.1 %fusion.76 = bf16[16,512,256]{1,2,0:T(8,128)(2,1)} fusion(bf16[16,512,256]{1,2,0:T(8,128)(2,1)} %get-tuple-element.293, s32[]{:T(128)} %get-tuple-element.292, bf16[512,3584]{1,0:T(8,128)(2,1)} %get-tuple-element.308, s32[3584]{0:T(1024)S(1)} %get-tuple-element.267, s32[3584]{0:T(1024)S(1)} %get-tuple-element.268, ...), kind=kOutput, calls=%fused_computation.16.clone.1 | convolution fusion | flops 942800896 | bytes 4223492 | tf_op jit(solution)/shard_map/while/body/eval_jaxpr/dot_general | solution.py:25
  75.2 0.9 dynamic-slice_reduce_fusion.2
  76.2 6.1 %fusion.76 = bf16[16,512,256]{1,2,0:T(8,128)(2,1)} fusion(bf16[16,512,256]{1,2,0:T(8,128)(2,1)} %get-tuple-element.293, s32[]{:T(128)} %get-tuple-element.292, bf16[512,3584]{1,0:T(8,128)(2,1)} %get-tuple-element.308, s32[3584]{0:T(1024)S(1)} %get-tuple-element.267, s32[3584]{0:T(1024)S(1)} %get-tuple-element.268, ...), kind=kOutput, calls=%fused_computation.16.clone.1 | convolution fusion | flops 942800896 | bytes 4223492 | tf_op jit(solution)/shard_map/while/body/eval_jaxpr/dot_general | solution.py:25
  85.1 0.9 dynamic-slice_reduce_fusion.2
  86.1 6.1 %fusion.76 = bf16[16,512,256]{1,2,0:T(8,128)(2,1)} fusion(bf16[16,512,256]{1,2,0:T(8,128)(2,1)} %get-tuple-element.293, s32[]{:T(128)} %get-tuple-element.292, bf16[512,3584]{1,0:T(8,128)(2,1)} %get-tuple-element.308, s32[3584]{0:T(1024)S(1)} %get-tuple-element.267, s32[3584]{0:T(1024)S(1)} %get-tuple-element.268, ...), kind=kOutput, calls=%fused_computation.16.clone.1 | convolution fusion | flops 942800896 | bytes 4223492 | tf_op jit(solution)/shard_map/while/body/eval_jaxpr/dot_general | solution.py:25
  95.0 0.9 dynamic-slice_reduce_fusion.2
  96.0 6.1 %fusion.76 = bf16[16,512,256]{1,2,0:T(8,128)(2,1)} fusion(bf16[16,512,256]{1,2,0:T(8,128)(2,1)} %get-tuple-element.293, s32[]{:T(128)} %get-tuple-element.292, bf16[512,3584]{1,0:T(8,128)(2,1)} %get-tuple-element.308, s32[3584]{0:T(1024)S(1)} %get-tuple-element.267, s32[3584]{0:T(1024)S(1)} %get-tuple-element.268, ...), kind=kOutput, calls=%fused_computation.16.clone.1 | convolution fusion | flops 942800896 | bytes 4223492 | tf_op jit(solution)/shard_map/while/body/eval_jaxpr/dot_general | solution.py:25
  104.9 0.9 dynamic-slice_reduce_fusion.2
  105.9 6.1 %fusion.76 = bf16[16,512,256]{1,2,0:T(8,128)(2,1)} fusion(bf16[16,512,256]{1,2,0:T(8,128)(2,1)} %get-tuple-element.293, s32[]{:T(128)} %get-tuple-element.292, bf16[512,3584]{1,0:T(8,128)(2,1)} %get-tuple-element.308, s32[3584]{0:T(1024)S(1)} %get-tuple-element.267, s32[3584]{0:T(1024)S(1)} %get-tuple-element.268, ...), kind=kOutput, calls=%fused_computation.16.clone.1 | convolution fusion | flops 942800896 | bytes 4223492 | tf_op jit(solution)/shard_map/while/body/eval_jaxpr/dot_general | solution.py:25
  114.8 0.9 dynamic-slice_reduce_fusion.2
  115.7 6.1 %fusion.76 = bf16[16,512,256]{1,2,0:T(8,128)(2,1)} fusion(bf16[16,512,256]{1,2,0:T(8,128)(2,1)} %get-tuple-element.293, s32[]{:T(128)} %get-tuple-element.292, bf16[512,3584]{1,0:T(8,128)(2,1)} %get-tuple-element.308, s32[3584]{0:T(1024)S(1)} %get-tuple-element.267, s32[3584]{0:T(1024)S(1)} %get-tuple-element.268, ...), kind=kOutput, calls=%fused_computation.16.clone.1 | convolution fusion | flops 942800896 | bytes 4223492 | tf_op jit(solution)/shard_map/while/body/eval_jaxpr/dot_general | solution.py:25
  124.7 0.9 dynamic-slice_reduce_fusion.2
  125.6 6.1 %fusion.76 = bf16[16,512,256]{1,2,0:T(8,128)(2,1)} fusion(bf16[16,512,256]{1,2,0:T(8,128)(2,1)} %get-tuple-element.293, s32[]{:T(128)} %get-tuple-element.292, bf16[512,3584]{1,0:T(8,128)(2,1)} %get-tuple-element.308, s32[3584]{0:T(1024)S(1)} %get-tuple-element.267, s32[3584]{0:T(1024)S(1)} %get-tuple-element.268, ...), kind=kOutput, calls=%fused_computation.16.clone.1 | convolution fusion | flops 942800896 | bytes 4223492 | tf_op jit(solution)/shard_map/while/body/eval_jaxpr/dot_general | solution.py:25
  134.6 0.9 dynamic-slice_reduce_fusion.2
  135.6 6.1 %fusion.76 = bf16[16,512,256]{1,2,0:T(8,128)(2,1)} fusion(bf16[16,512,256]{1,2,0:T(8,128)(2,1)} %get-tuple-element.293, s32[]{:T(128)} %get-tuple-element.292, bf16[512,3584]{1,0:T(8,128)(2,1)} %get-tuple-element.308, s32[3584]{0:T(1024)S(1)} %get-tuple-element.267, s32[3584]{0:T(1024)S(1)} %get-tuple-element.268, ...), kind=kOutput, calls=%fused_computation.16.clone.1 | convolution fusion | flops 942800896 | bytes 4223492 | tf_op jit(solution)/shard_map/while/body/eval_jaxpr/dot_general | solution.py:25
  144.5 0.9 dynamic-slice_reduce_fusion.2
  145.4 6.1 %fusion.76 = bf16[16,512,256]{1,2,0:T(8,128)(2,1)} fusion(bf16[16,512,256]{1,2,0:T(8,128)(2,1)} %get-tuple-element.293, s32[]{:T(128)} %get-tuple-element.292, bf16[512,3584]{1,0:T(8,128)(2,1)} %get-tuple-element.308, s32[3584]{0:T(1024)S(1)} %get-tuple-element.267, s32[3584]{0:T(1024)S(1)} %get-tuple-element.268, ...), kind=kOutput, calls=%fused_computation.16.clone.1 | convolution fusion | flops 942800896 | bytes 4223492 | tf_op jit(solution)/shard_map/while/body/eval_jaxpr/dot_general | solution.py:25
  154.3 0.9 dynamic-slice_reduce_fusion.2
  155.3 6.1 %fusion.76 = bf16[16,512,256]{1,2,0:T(8,128)(2,1)} fusion(bf16[16,512,256]{1,2,0:T(8,128)(2,1)} %get-tuple-element.293, s32[]{:T(128)} %get-tuple-element.292, bf16[512,3584]{1,0:T(8,128)(2,1)} %get-tuple-element.308, s32[3584]{0:T(1024)S(1)} %get-tuple-element.267, s32[3584]{0:T(1024)S(1)} %get-tuple-element.268, ...), kind=kOutput, calls=%fused_computation.16.clone.1 | convolution fusion | flops 942800896 | bytes 4223492 | tf_op jit(solution)/shard_map/while/body/eval_jaxpr/dot_general | solution.py:25
  164.2 0.9 dynamic-slice_reduce_fusion.2
  165.2 6.1 %fusion.76 = bf16[16,512,256]{1,2,0:T(8,128)(2,1)} fusion(bf16[16,512,256]{1,2,0:T(8,128)(2,1)} %get-tuple-element.293, s32[]{:T(128)} %get-tuple-element.292, bf16[512,3584]{1,0:T(8,128)(2,1)} %get-tuple-element.308, s32[3584]{0:T(1024)S(1)} %get-tuple-element.267, s32[3584]{0:T(1024)S(1)} %get-tuple-element.268, ...), kind=kOutput, calls=%fused_computation.16.clone.1 | convolution fusion | flops 942800896 | bytes 4223492 | tf_op jit(solution)/shard_map/while/body/eval_jaxpr/dot_general | solution.py:25
  171.3 4.6 convolution_bitcast_fusion
  176.0 6.7 %fusion.17 = f32[16,256,256]{1,2,0:T(8,128)} fusion(bf16[16,512,256]{1,2,0:T(8,128)(2,1)} %get-tuple-element.99, bf16[512]{0:T(512)(128)(2,1)S(1)} %convert_element_type.36), kind=kOutput, calls=%fused_computation.29 | convolution fusion | flops 1075838976 | bytes 8389632 | tf_op jit(solution)/shard_map/htk,htj->hkj/dot_general | solution.py:48
  183.4 24.0 %psum.14 = f32[]{:T(128)} all-reduce(f32[]{:T(128)} %convert_reduce_fusion), channel_id=1, replica_groups=mesh['seq'=8,'rep'=4] {'seq'}, use_global_device_ids=true, to_apply=%region_4.5 | all-reduce | flops 1 | bytes 8 | tf_op jit(solution)/shard_map/psum | solution.py:47
  208.0 34.9 %reduce-scatter.6.cloned.1.call-done = f32[2,64,256]{2,1,0:T(8,128)} async-done(((f32[16,64,256]{2,1,0:T(8,128)}), f32[2,64,256]{2,1,0:T(8,128)}) %reduce-scatter.6.cloned.1.call-update) | async-done | bytes 131088 | tf_op jit(solution)/shard_map/reduce_scatter | solution.py:63
  242.9 0.9 slice_bitcast_fusion.4
  243.8 90.0 %reduce-scatter.4.cloned.1.call-done = f32[2,256,256]{1,2,0:T(8,128)} async-done(((f32[16,256,256]{1,2,0:T(8,128)}), f32[2,256,256]{1,2,0:T(8,128)}) %reduce-scatter.4.cloned.1.call-update) | async-done | bytes 524304 | tf_op jit(solution)/shard_map/reduce_scatter | solution.py:62
  333.8 1.1 select_add_fusion.1
  335.3 11.7 %cholesky.130 = f32[128,128]{1,0:T(8,128)S(1)} custom-call(f32[128,128]{1,0:T(8,128)S(1)} %cholesky.194), custom_call_target="Cholesky" | custom-call | tf_op jit(solution)/shard_map/jit(cholesky)/cholesky | solution.py:37
  347.0 9.8 %custom-call.15 = f32[1,128,128]{1,2,0:T(8,128)S(1)} custom-call(f32[1,128,128]{2,1,0:T(8,128)S(1)} %get-tuple-element.171), custom_call_target="InvertDiagBlocksLowerTriangular" | custom-call | tf_op jit(solution)/shard_map/jit(cholesky)/cholesky | solution.py:37
  357.3 11.7 %cholesky.147 = f32[128,128]{1,0:T(8,128)S(1)} custom-call(f32[128,128]{1,0:T(8,128)S(1)} %convolution_subtract_fusion.1), custom_call_target="Cholesky" | custom-call | tf_op jit(solution)/shard_map/jit(cholesky)/cholesky | solution.py:37
  371.7 3.7 while.18
  372.3 1.3 bitcast_dynamic-update-slice_fusion.4
  374.1 1.3 bitcast_dynamic-update-slice_fusion.4
  375.4 19.9 %custom-call.16 = f32[2,128,128]{1,2,0:T(8,128)S(1)} custom-call(f32[2,128,128]{2,1,0:T(8,128)S(1)} %get-tuple-element.128), custom_call_target="InvertDiagBlocksLowerTriangular" | custom-call | tf_op jit(solution)/shard_map/jit(_cho_solve)/triangular_solve | solution.py:38
  396.8 11.7 %cholesky.164 = f32[128,128]{1,0:T(8,128)S(1)} custom-call(f32[128,128]{1,0:T(8,128)S(1)} %cholesky.197), custom_call_target="Cholesky" | custom-call | tf_op jit(solution)/shard_map/jit(cholesky)/cholesky | solution.py:37
  408.6 9.8 %custom-call.17 = f32[1,128,128]{1,2,0:T(8,128)S(1)} custom-call(f32[1,128,128]{2,1,0:T(8,128)S(1)} %get-tuple-element.175), custom_call_target="InvertDiagBlocksLowerTriangular" | custom-call | tf_op jit(solution)/shard_map/jit(cholesky)/cholesky | solution.py:37
  418.9 11.7 %cholesky.181 = f32[128,128]{1,0:T(8,128)S(1)} custom-call(f32[128,128]{1,0:T(8,128)S(1)} %convolution_subtract_fusion), custom_call_target="Cholesky" | custom-call | tf_op jit(solution)/shard_map/jit(cholesky)/cholesky | solution.py:37
  431.3 0.7 compare_reduce_fusion.1
  433.3 4.1 while.19
  433.3 0.7 fusion.78
  434.0 1.3 bitcast_dynamic-update-slice_fusion.5
  435.4 0.7 fusion.78
  436.0 1.3 bitcast_dynamic-update-slice_fusion.5
  437.4 19.9 %custom-call.18 = f32[2,128,128]{1,2,0:T(8,128)S(1)} custom-call(f32[2,128,128]{2,1,0:T(8,128)S(1)} %get-tuple-element.129), custom_call_target="InvertDiagBlocksLowerTriangular" | custom-call | tf_op jit(solution)/shard_map/jit(_cho_solve)/triangular_solve | solution.py:38
  458.8 31.4 %all_gather.3 = bf16[16,256,64]{1,2,0:T(8,128)(2,1)S(1)} all-gather(bf16[2,256,64]{1,2,0:T(8,128)(2,1)S(1)} %pad_maximum_fusion), channel_id=1, replica_groups=mesh['seq'=8,'rep'=4] {'seq'}, dimensions={0}, use_global_device_ids=true | all-gather | bytes 589824 | tf_op jit(solution)/shard_map/all_gather | solution.py:71
  490.2 3.7 convolution_bitcast_fusion.1
  494.0 19.3 %reduce-scatter.8.cloned.1.call-done = f32[128,64]{0,1:T(8,128)} async-done(((f32[512,64]{0,1:T(8,128)}), f32[128,64]{0,1:T(8,128)}) %reduce-scatter.8.cloned.1.call-update) | async-done | bytes 32784 | tf_op jit(solution)/shard_map/reduce_scatter | solution.py:73
  513.3 0.9 fusion.45
  514.1 39.3 %psum.15 = f32[64]{0:T(128)S(1)} all-reduce(f32[64]{0:T(128)S(1)} %fusion.45), channel_id=1, replica_groups=mesh['seq'=8,'rep'=4] {'seq','rep'}, use_global_device_ids=true, to_apply=%region_12.15 | all-reduce | flops 64 | bytes 512 | tf_op jit(solution)/shard_map/psum | solution.py:77
  553.4 1.5 broadcast_divide_fusion
  (94 shorter events, 17.6 us)
Async XLA Ops:
  6.5 236.4 %reduce-scatter.6.cloned.1.call-start = ((), (), s32[]{:S(2)}) async-start(), calls=%async_computation.4 | async-start | bytes 1179648 | tf_op jit(solution)/shard_map/reduce_scatter | solution.py:63
  13.0 158.3 %copy-start.1 = (s32[64]{0:T(128)S(1)}, s32[64]{0:T(128)}, u32[]{:S(2)}) copy-start(s32[64]{0:T(128)} %param.14) | copy-start | bytes 772
  171.3 4.7 copy-start
  176.0 157.9 %reduce-scatter.4.cloned.1.call-start = ((), (), s32[]{:S(2)}) async-start(), calls=%async_computation.3 | async-start | bytes 4718592 | tf_op jit(solution)/shard_map/reduce_scatter | solution.py:62
  182.8 330.5 %reduce-scatter.8.cloned.1.call-start = ((), (), s32[]{:S(2)}) async-start(), calls=%async_computation.5 | async-start | bytes 163840 | tf_op jit(solution)/shard_map/reduce_scatter | solution.py:73
Sparse Core Ops, SparseCore 0:
  176.1 66.8 reduce-scatter.5
  246.6 87.2 reduce-scatter.3
  494.0 19.2 reduce-scatter.7
where the time goes:
time: 564 us; the launch traced here: 561 us
  waiting for transfers between devices  144 us (26%)
  matrix products  116 us (21%)
  other arithmetic  114 us (20%)
  blocking collectives  94.6 us (17%)
  local copies, waits for them, and re-layouts  39.5 us (7%)
  loops' own time  36.8 us (7%)
  between operations  16.5 us (3%)
    dot_general x16, matrix products, one_head(): counted = jnp.dot(gradient, count_table, preferred_element_type=jnp.float32)  97.2 us
    reduce_scatter x1, waiting for transfers between devices, on_device(): lax.psum_scatter(local_grams, 'seq', scatter_dimension=0, tiled=True)  90 us
    another operation x14, other arithmetic, solve_queries(): factor = jnp.linalg.cholesky(gram_sum)  69.2 us
    another operation x5, other arithmetic, solve_queries(): jax.scipy.linalg.cho_solve((factor, True), chosen.T).astype(jnp.bfloat16)  39.9 us
    psum x1, blocking collectives, on_device(): norm_sum = lax.psum(partial_value, ('seq', 'rep')) / token_count  39.3 us
    another operation x1, loops' own time, build_sketches(): return lax.map(one_head, jnp.arange(head_count, dtype=jnp.int32))  36.7 us
    reduce_scatter x1, waiting for transfers between devices, on_device(): lax.psum_scatter(local_chosen, 'seq', scatter_dimension=0, tiled=True)  34.9 us
    all_gather x1, blocking collectives, on_device(): solved_all = lax.all_gather(solved, 'seq', axis=0, tiled=True)  31.4 us
  transfers between devices with their start and end apart: 3, of which 3 were waited for; matrix products, arithmetic and copies ran while one was open for 1% of the time, Pallas kernels for 0%

commit v1 on v0

--- a/solution.py
+++ b/solution.py
@@ -74,7 +74,7 @@
     row_start = lax.axis_index("rep") * out_rows
     mask_rows = lax.dynamic_slice_in_dim(loss_mask, row_start, out_rows, 0).astype(jnp.float32)
     partial_value = jnp.sum(mask_rows[:, None] * contrib * contrib, 0)
-    norm_sum = lax.psum(partial_value, ("seq", "rep")) / token_count
+    norm_sum = lax.psum(lax.psum(partial_value, "rep"), "seq") / token_count
     return contrib / jnp.sqrt(norm_sum + norm_floor)
 
 

time: 564 us -> 552 us (0.979)
  blocking collectives: 94.6 us -> 82.6 us
    psum x1 -> x2, blocking collectives: 39.3 us -> 27.3 us  [on_device(): norm_sum = lax.psum(lax.psum(partial_value, 'rep'), 'seq') / token_count]
  transfers between devices with their start and end apart: 3 -> 3, of which waited for: 3 -> 3; matrix products, arithmetic and copies ran while one was open for 1% -> 2% of each run, Pallas kernels for 0% -> 0%
where the time goes in v1:
time: 552 us; the launch traced here: 549 us
  waiting for transfers between devices  144 us (26%)
  matrix products  116 us (21%)
  other arithmetic  114 us (21%)
  blocking collectives  82.6 us (15%)
  local copies, waits for them, and re-layouts  39.5 us (7%)
  loops' own time  36.8 us (7%)
  between operations  16.5 us (3%)
    dot_general x16, matrix products, one_head(): counted = jnp.dot(gradient, count_table, preferred_element_type=jnp.float32)  97.2 us
    reduce_scatter x1, waiting for transfers between devices, on_device(): lax.psum_scatter(local_grams, 'seq', scatter_dimension=0, tiled=True)  90 us
    another operation x14, other arithmetic, solve_queries(): factor = jnp.linalg.cholesky(gram_sum)  69.2 us
    another operation x5, other arithmetic, solve_queries(): jax.scipy.linalg.cho_solve((factor, True), chosen.T).astype(jnp.bfloat16)  39.9 us
    another operation x1, loops' own time, build_sketches(): return lax.map(one_head, jnp.arange(head_count, dtype=jnp.int32))  36.7 us
    reduce_scatter x1, waiting for transfers between devices, on_device(): lax.psum_scatter(local_chosen, 'seq', scatter_dimension=0, tiled=True)  34.9 us
    all_gather x1, blocking collectives, on_device(): solved_all = lax.all_gather(solved, 'seq', axis=0, tiled=True)  31.4 us
    psum x2, blocking collectives, on_device(): norm_sum = lax.psum(lax.psum(partial_value, 'rep'), 'seq') / token_count  27.3 us
  transfers between devices with their start and end apart: 3, of which 3 were waited for; matrix products, arithmetic and copies ran while one was open for 2% of the time, Pallas kernels for 0%

profile of v1, /device:TPU:0, one launch (start us, length us, event | category | flops | bytes accessed | tf_op | source)
XLA Modules:
  0.0 549.4 jit_solution(14898958786919069979)
XLA Ops:
  6.5 6.5 %copy.13 = bf16[1,512,4096]{1,2,0:T(8,128)(2,1)} copy(bf16[1,512,4096]{2,1,0:T(8,128)(2,1)} %param.10) | data formatting | bytes 8388608 | tf_op args[0]
  13.0 158.3 %while.17 = (s32[]{:T(128)}, bf16[16,512,256]{1,2,0:T(8,128)(2,1)}, s32[16]{0:T(128)S(1)}, bf16[512,4096]{0,1:T(8,128)(2,1)}, s32[16,3584]{1,0:T(8,128)}, /*inde...) while((s32[]{:T(128)}, bf16[16,512,256]{1,2,0:T(8,128)(2,1)}, ...), condition=%wide.region_1.2_spmd.clone, body=%wide.region_0.1_spmd.clone.sunk | while | flops 942876160 | bytes 4295377 | solution.py:31
  15.8 0.9 dynamic-slice_reduce_fusion.2
  16.8 6.1 %fusion.76 = bf16[16,512,256]{1,2,0:T(8,128)(2,1)} fusion(bf16[16,512,256]{1,2,0:T(8,128)(2,1)} %get-tuple-element.293, s32[]{:T(128)} %get-tuple-element.292, bf16[512,3584]{1,0:T(8,128)(2,1)} %get-tuple-element.308, s32[3584]{0:T(1024)S(1)} %get-tuple-element.267, s32[3584]{0:T(1024)S(1)} %get-tuple-element.268, ...), kind=kOutput, calls=%fused_computation.16.clone.1 | convolution fusion | flops 942800896 | bytes 4223492 | tf_op jit(solution)/shard_map/while/body/eval_jaxpr/dot_general | solution.py:25
  25.7 0.9 dynamic-slice_reduce_fusion.2
  26.7 6.1 %fusion.76 = bf16[16,512,256]{1,2,0:T(8,128)(2,1)} fusion(bf16[16,512,256]{1,2,0:T(8,128)(2,1)} %get-tuple-element.293, s32[]{:T(128)} %get-tuple-element.292, bf16[512,3584]{1,0:T(8,128)(2,1)} %get-tuple-element.308, s32[3584]{0:T(1024)S(1)} %get-tuple-element.267, s32[3584]{0:T(1024)S(1)} %get-tuple-element.268, ...), kind=kOutput, calls=%fused_computation.16.clone.1 | convolution fusion | flops 942800896 | bytes 4223492 | tf_op jit(solution)/shard_map/while/body/eval_jaxpr/dot_general | solution.py:25
  35.6 0.9 dynamic-slice_reduce_fusion.2
  36.6 6.1 %fusion.76 = bf16[16,512,256]{1,2,0:T(8,128)(2,1)} fusion(bf16[16,512,256]{1,2,0:T(8,128)(2,1)} %get-tuple-element.293, s32[]{:T(128)} %get-tuple-element.292, bf16[512,3584]{1,0:T(8,128)(2,1)} %get-tuple-element.308, s32[3584]{0:T(1024)S(1)} %get-tuple-element.267, s32[3584]{0:T(1024)S(1)} %get-tuple-element.268, ...), kind=kOutput, calls=%fused_computation.16.clone.1 | convolution fusion | flops 942800896 | bytes 4223492 | tf_op jit(solution)/shard_map/while/body/eval_jaxpr/dot_general | solution.py:25
  45.5 0.9 dynamic-slice_reduce_fusion.2
  46.5 6.1 %fusion.76 = bf16[16,512,256]{1,2,0:T(8,128)(2,1)} fusion(bf16[16,512,256]{1,2,0:T(8,128)(2,1)} %get-tuple-element.293, s32[]{:T(128)} %get-tuple-element.292, bf16[512,3584]{1,0:T(8,128)(2,1)} %get-tuple-element.308, s32[3584]{0:T(1024)S(1)} %get-tuple-element.267, s32[3584]{0:T(1024)S(1)} %get-tuple-element.268, ...), kind=kOutput, calls=%fused_computation.16.clone.1 | convolution fusion | flops 942800896 | bytes 4223492 | tf_op jit(solution)/shard_map/while/body/eval_jaxpr/dot_general | solution.py:25
  55.4 0.9 dynamic-slice_reduce_fusion.2
  56.4 6.1 %fusion.76 = bf16[16,512,256]{1,2,0:T(8,128)(2,1)} fusion(bf16[16,512,256]{1,2,0:T(8,128)(2,1)} %get-tuple-element.293, s32[]{:T(128)} %get-tuple-element.292, bf16[512,3584]{1,0:T(8,128)(2,1)} %get-tuple-element.308, s32[3584]{0:T(1024)S(1)} %get-tuple-element.267, s32[3584]{0:T(1024)S(1)} %get-tuple-element.268, ...), kind=kOutput, calls=%fused_computation.16.clone.1 | convolution fusion | flops 942800896 | bytes 4223492 | tf_op jit(solution)/shard_map/while/body/eval_jaxpr/dot_general | solution.py:25
  65.3 0.9 dynamic-slice_reduce_fusion.2
  66.3 6.1 %fusion.76 = bf16[16,512,256]{1,2,0:T(8,128)(2,1)} fusion(bf16[16,512,256]{1,2,0:T(8,128)(2,1)} %get-tuple-element.293, s32[]{:T(128)} %get-tuple-element.292, bf16[512,3584]{1,0:T(8,128)(2,1)} %get-tuple-element.308, s32[3584]{0:T(1024)S(1)} %get-tuple-element.267, s32[3584]{0:T(1024)S(1)} %get-tuple-element.268, ...), kind=kOutput, calls=%fused_computation.16.clone.1 | convolution fusion | flops 942800896 | bytes 4223492 | tf_op jit(solution)/shard_map/while/body/eval_jaxpr/dot_general | solution.py:25
  75.2 0.9 dynamic-slice_reduce_fusion.2
  76.2 6.1 %fusion.76 = bf16[16,512,256]{1,2,0:T(8,128)(2,1)} fusion(bf16[16,512,256]{1,2,0:T(8,128)(2,1)} %get-tuple-element.293, s32[]{:T(128)} %get-tuple-element.292, bf16[512,3584]{1,0:T(8,128)(2,1)} %get-tuple-element.308, s32[3584]{0:T(1024)S(1)} %get-tuple-element.267, s32[3584]{0:T(1024)S(1)} %get-tuple-element.268, ...), kind=kOutput, calls=%fused_computation.16.clone.1 | convolution fusion | flops 942800896 | bytes 4223492 | tf_op jit(solution)/shard_map/while/body/eval_jaxpr/dot_general | solution.py:25
  85.1 0.9 dynamic-slice_reduce_fusion.2
  86.1 6.1 %fusion.76 = bf16[16,512,256]{1,2,0:T(8,128)(2,1)} fusion(bf16[16,512,256]{1,2,0:T(8,128)(2,1)} %get-tuple-element.293, s32[]{:T(128)} %get-tuple-element.292, bf16[512,3584]{1,0:T(8,128)(2,1)} %get-tuple-element.308, s32[3584]{0:T(1024)S(1)} %get-tuple-element.267, s32[3584]{0:T(1024)S(1)} %get-tuple-element.268, ...), kind=kOutput, calls=%fused_computation.16.clone.1 | convolution fusion | flops 942800896 | bytes 4223492 | tf_op jit(solution)/shard_map/while/body/eval_jaxpr/dot_general | solution.py:25
  95.0 0.9 dynamic-slice_reduce_fusion.2
  96.0 6.1 %fusion.76 = bf16[16,512,256]{1,2,0:T(8,128)(2,1)} fusion(bf16[16,512,256]{1,2,0:T(8,128)(2,1)} %get-tuple-element.293, s32[]{:T(128)} %get-tuple-element.292, bf16[512,3584]{1,0:T(8,128)(2,1)} %get-tuple-element.308, s32[3584]{0:T(1024)S(1)} %get-tuple-element.267, s32[3584]{0:T(1024)S(1)} %get-tuple-element.268, ...), kind=kOutput, calls=%fused_computation.16.clone.1 | convolution fusion | flops 942800896 | bytes 4223492 | tf_op jit(solution)/shard_map/while/body/eval_jaxpr/dot_general | solution.py:25
  104.9 0.9 dynamic-slice_reduce_fusion.2
  105.9 6.1 %fusion.76 = bf16[16,512,256]{1,2,0:T(8,128)(2,1)} fusion(bf16[16,512,256]{1,2,0:T(8,128)(2,1)} %get-tuple-element.293, s32[]{:T(128)} %get-tuple-element.292, bf16[512,3584]{1,0:T(8,128)(2,1)} %get-tuple-element.308, s32[3584]{0:T(1024)S(1)} %get-tuple-element.267, s32[3584]{0:T(1024)S(1)} %get-tuple-element.268, ...), kind=kOutput, calls=%fused_computation.16.clone.1 | convolution fusion | flops 942800896 | bytes 4223492 | tf_op jit(solution)/shard_map/while/body/eval_jaxpr/dot_general | solution.py:25
  114.8 0.9 dynamic-slice_reduce_fusion.2
  115.7 6.1 %fusion.76 = bf16[16,512,256]{1,2,0:T(8,128)(2,1)} fusion(bf16[16,512,256]{1,2,0:T(8,128)(2,1)} %get-tuple-element.293, s32[]{:T(128)} %get-tuple-element.292, bf16[512,3584]{1,0:T(8,128)(2,1)} %get-tuple-element.308, s32[3584]{0:T(1024)S(1)} %get-tuple-element.267, s32[3584]{0:T(1024)S(1)} %get-tuple-element.268, ...), kind=kOutput, calls=%fused_computation.16.clone.1 | convolution fusion | flops 942800896 | bytes 4223492 | tf_op jit(solution)/shard_map/while/body/eval_jaxpr/dot_general | solution.py:25
  124.7 0.9 dynamic-slice_reduce_fusion.2
  125.6 6.1 %fusion.76 = bf16[16,512,256]{1,2,0:T(8,128)(2,1)} fusion(bf16[16,512,256]{1,2,0:T(8,128)(2,1)} %get-tuple-element.293, s32[]{:T(128)} %get-tuple-element.292, bf16[512,3584]{1,0:T(8,128)(2,1)} %get-tuple-element.308, s32[3584]{0:T(1024)S(1)} %get-tuple-element.267, s32[3584]{0:T(1024)S(1)} %get-tuple-element.268, ...), kind=kOutput, calls=%fused_computation.16.clone.1 | convolution fusion | flops 942800896 | bytes 4223492 | tf_op jit(solution)/shard_map/while/body/eval_jaxpr/dot_general | solution.py:25
  134.6 0.9 dynamic-slice_reduce_fusion.2
  135.6 6.1 %fusion.76 = bf16[16,512,256]{1,2,0:T(8,128)(2,1)} fusion(bf16[16,512,256]{1,2,0:T(8,128)(2,1)} %get-tuple-element.293, s32[]{:T(128)} %get-tuple-element.292, bf16[512,3584]{1,0:T(8,128)(2,1)} %get-tuple-element.308, s32[3584]{0:T(1024)S(1)} %get-tuple-element.267, s32[3584]{0:T(1024)S(1)} %get-tuple-element.268, ...), kind=kOutput, calls=%fused_computation.16.clone.1 | convolution fusion | flops 942800896 | bytes 4223492 | tf_op jit(solution)/shard_map/while/body/eval_jaxpr/dot_general | solution.py:25
  144.5 0.9 dynamic-slice_reduce_fusion.2
  145.4 6.1 %fusion.76 = bf16[16,512,256]{1,2,0:T(8,128)(2,1)} fusion(bf16[16,512,256]{1,2,0:T(8,128)(2,1)} %get-tuple-element.293, s32[]{:T(128)} %get-tuple-element.292, bf16[512,3584]{1,0:T(8,128)(2,1)} %get-tuple-element.308, s32[3584]{0:T(1024)S(1)} %get-tuple-element.267, s32[3584]{0:T(1024)S(1)} %get-tuple-element.268, ...), kind=kOutput, calls=%fused_computation.16.clone.1 | convolution fusion | flops 942800896 | bytes 4223492 | tf_op jit(solution)/shard_map/while/body/eval_jaxpr/dot_general | solution.py:25
  154.3 0.9 dynamic-slice_reduce_fusion.2
  155.3 6.1 %fusion.76 = bf16[16,512,256]{1,2,0:T(8,128)(2,1)} fusion(bf16[16,512,256]{1,2,0:T(8,128)(2,1)} %get-tuple-element.293, s32[]{:T(128)} %get-tuple-element.292, bf16[512,3584]{1,0:T(8,128)(2,1)} %get-tuple-element.308, s32[3584]{0:T(1024)S(1)} %get-tuple-element.267, s32[3584]{0:T(1024)S(1)} %get-tuple-element.268, ...), kind=kOutput, calls=%fused_computation.16.clone.1 | convolution fusion | flops 942800896 | bytes 4223492 | tf_op jit(solution)/shard_map/while/body/eval_jaxpr/dot_general | solution.py:25
  164.2 0.9 dynamic-slice_reduce_fusion.2
  165.2 6.1 %fusion.76 = bf16[16,512,256]{1,2,0:T(8,128)(2,1)} fusion(bf16[16,512,256]{1,2,0:T(8,128)(2,1)} %get-tuple-element.293, s32[]{:T(128)} %get-tuple-element.292, bf16[512,3584]{1,0:T(8,128)(2,1)} %get-tuple-element.308, s32[3584]{0:T(1024)S(1)} %get-tuple-element.267, s32[3584]{0:T(1024)S(1)} %get-tuple-element.268, ...), kind=kOutput, calls=%fused_computation.16.clone.1 | convolution fusion | flops 942800896 | bytes 4223492 | tf_op jit(solution)/shard_map/while/body/eval_jaxpr/dot_general | solution.py:25
  171.3 4.6 convolution_bitcast_fusion
  176.0 6.7 %fusion.17 = f32[16,256,256]{1,2,0:T(8,128)} fusion(bf16[16,512,256]{1,2,0:T(8,128)(2,1)} %get-tuple-element.99, bf16[512]{0:T(512)(128)(2,1)S(1)} %convert_element_type.36), kind=kOutput, calls=%fused_computation.29 | convolution fusion | flops 1075838976 | bytes 8389632 | tf_op jit(solution)/shard_map/htk,htj->hkj/dot_general | solution.py:48
  183.4 24.0 %psum.21 = f32[]{:T(128)} all-reduce(f32[]{:T(128)} %convert_reduce_fusion), channel_id=1, replica_groups=mesh['seq'=8,'rep'=4] {'seq'}, use_global_device_ids=true, to_apply=%region_4.5 | all-reduce | flops 1 | bytes 8 | tf_op jit(solution)/shard_map/psum | solution.py:47
  208.0 34.9 %reduce-scatter.6.cloned.1.call-done = f32[2,64,256]{2,1,0:T(8,128)} async-done(((f32[16,64,256]{2,1,0:T(8,128)}), f32[2,64,256]{2,1,0:T(8,128)}) %reduce-scatter.6.cloned.1.call-update) | async-done | bytes 131088 | tf_op jit(solution)/shard_map/reduce_scatter | solution.py:63
  242.9 0.9 slice_bitcast_fusion.4
  243.8 90.0 %reduce-scatter.4.cloned.1.call-done = f32[2,256,256]{1,2,0:T(8,128)} async-done(((f32[16,256,256]{1,2,0:T(8,128)}), f32[2,256,256]{1,2,0:T(8,128)}) %reduce-scatter.4.cloned.1.call-update) | async-done | bytes 524304 | tf_op jit(solution)/shard_map/reduce_scatter | solution.py:62
  333.8 1.1 select_add_fusion.1
  335.3 11.7 %cholesky.130 = f32[128,128]{1,0:T(8,128)S(1)} custom-call(f32[128,128]{1,0:T(8,128)S(1)} %cholesky.194), custom_call_target="Cholesky" | custom-call | tf_op jit(solution)/shard_map/jit(cholesky)/cholesky | solution.py:37
  347.0 9.8 %custom-call.15 = f32[1,128,128]{1,2,0:T(8,128)S(1)} custom-call(f32[1,128,128]{2,1,0:T(8,128)S(1)} %get-tuple-element.171), custom_call_target="InvertDiagBlocksLowerTriangular" | custom-call | tf_op jit(solution)/shard_map/jit(cholesky)/cholesky | solution.py:37
  357.3 11.7 %cholesky.147 = f32[128,128]{1,0:T(8,128)S(1)} custom-call(f32[128,128]{1,0:T(8,128)S(1)} %convolution_subtract_fusion.1), custom_call_target="Cholesky" | custom-call | tf_op jit(solution)/shard_map/jit(cholesky)/cholesky | solution.py:37
  371.7 3.7 while.18
  372.3 1.3 bitcast_dynamic-update-slice_fusion.4
  374.1 1.3 bitcast_dynamic-update-slice_fusion.4
  375.4 19.9 %custom-call.16 = f32[2,128,128]{1,2,0:T(8,128)S(1)} custom-call(f32[2,128,128]{2,1,0:T(8,128)S(1)} %get-tuple-element.128), custom_call_target="InvertDiagBlocksLowerTriangular" | custom-call | tf_op jit(solution)/shard_map/jit(_cho_solve)/triangular_solve | solution.py:38
  396.8 11.7 %cholesky.164 = f32[128,128]{1,0:T(8,128)S(1)} custom-call(f32[128,128]{1,0:T(8,128)S(1)} %cholesky.197), custom_call_target="Cholesky" | custom-call | tf_op jit(solution)/shard_map/jit(cholesky)/cholesky | solution.py:37
  408.6 9.8 %custom-call.17 = f32[1,128,128]{1,2,0:T(8,128)S(1)} custom-call(f32[1,128,128]{2,1,0:T(8,128)S(1)} %get-tuple-element.175), custom_call_target="InvertDiagBlocksLowerTriangular" | custom-call | tf_op jit(solution)/shard_map/jit(cholesky)/cholesky | solution.py:37
  418.9 11.7 %cholesky.181 = f32[128,128]{1,0:T(8,128)S(1)} custom-call(f32[128,128]{1,0:T(8,128)S(1)} %convolution_subtract_fusion), custom_call_target="Cholesky" | custom-call | tf_op jit(solution)/shard_map/jit(cholesky)/cholesky | solution.py:37
  431.3 0.7 compare_reduce_fusion.1
  433.3 4.1 while.19
  433.3 0.7 fusion.78
  434.0 1.3 bitcast_dynamic-update-slice_fusion.5
  436.0 1.3 bitcast_dynamic-update-slice_fusion.5
  437.4 19.9 %custom-call.18 = f32[2,128,128]{1,2,0:T(8,128)S(1)} custom-call(f32[2,128,128]{2,1,0:T(8,128)S(1)} %get-tuple-element.129), custom_call_target="InvertDiagBlocksLowerTriangular" | custom-call | tf_op jit(solution)/shard_map/jit(_cho_solve)/triangular_solve | solution.py:38
  458.8 31.4 %all_gather.3 = bf16[16,256,64]{1,2,0:T(8,128)(2,1)S(1)} all-gather(bf16[2,256,64]{1,2,0:T(8,128)(2,1)S(1)} %pad_maximum_fusion), channel_id=1, replica_groups=mesh['seq'=8,'rep'=4] {'seq'}, dimensions={0}, use_global_device_ids=true | all-gather | bytes 589824 | tf_op jit(solution)/shard_map/all_gather | solution.py:71
  490.2 3.7 convolution_bitcast_fusion.1
  494.0 19.3 %reduce-scatter.8.cloned.1.call-done = f32[128,64]{0,1:T(8,128)} async-done(((f32[512,64]{0,1:T(8,128)}), f32[128,64]{0,1:T(8,128)}) %reduce-scatter.8.cloned.1.call-update) | async-done | bytes 32784 | tf_op jit(solution)/shard_map/reduce_scatter | solution.py:73
  513.3 0.9 fusion.45
  514.1 5.8 %psum.22 = f32[64]{0:T(128)S(1)} all-reduce(f32[64]{0:T(128)S(1)} %fusion.45), channel_id=1, replica_groups=mesh['seq'=8,'rep'=4] {'rep'}, use_global_device_ids=true, to_apply=%region_12.15 | all-reduce | flops 64 | bytes 512 | tf_op jit(solution)/shard_map/psum | solution.py:77
  519.9 21.5 %psum.23 = f32[64]{0:T(128)S(1)} all-reduce(f32[64]{0:T(128)S(1)} %psum.22), channel_id=1, replica_groups=mesh['seq'=8,'rep'=4] {'seq'}, use_global_device_ids=true, to_apply=%region_13.16 | all-reduce | flops 64 | bytes 512 | tf_op jit(solution)/shard_map/psum | solution.py:77
  541.4 1.5 broadcast_divide_fusion
  (95 shorter events, 18.2 us)
Async XLA Ops:
  6.5 236.4 %reduce-scatter.6.cloned.1.call-start = ((), (), s32[]{:S(2)}) async-start(), calls=%async_computation.4 | async-start | bytes 1179648 | tf_op jit(solution)/shard_map/reduce_scatter | solution.py:63
  13.0 158.3 %copy-start.1 = (s32[64]{0:T(128)S(1)}, s32[64]{0:T(128)}, u32[]{:S(2)}) copy-start(s32[64]{0:T(128)} %param.14) | copy-start | bytes 772
  171.3 4.7 copy-start
  176.0 157.9 %reduce-scatter.4.cloned.1.call-start = ((), (), s32[]{:S(2)}) async-start(), calls=%async_computation.3 | async-start | bytes 4718592 | tf_op jit(solution)/shard_map/reduce_scatter | solution.py:62
  182.8 330.5 %reduce-scatter.8.cloned.1.call-start = ((), (), s32[]{:S(2)}) async-start(), calls=%async_computation.5 | async-start | bytes 163840 | tf_op jit(solution)/shard_map/reduce_scatter | solution.py:73
Sparse Core Ops, SparseCore 0:
  176.1 66.8 reduce-scatter.5
  246.6 87.2 reduce-scatter.3
  494.0 19.2 reduce-scatter.7
